TPU v7x, 128 devices: a whole 4x4x4 slice. The times are simulated.
128 devices in a mesh: pi: 8 (over y, x_lo), pj: 16 (over x_hi, z, core).
Axes of the slice: x: 4 (x_hi: 2, x_lo: 2; x = x_hi * 2 + x_lo), y: 4, z: 4, core: 2. Of those that a mesh axis runs over, the one named last changes fastest.
Arguments:
- duo_embedding: bfloat16 [2048, 2048, 128], P('pi', 'pj'), may hold values from -12 to 12
- duo_attention_weights: float32 [128, 8], replicated, may hold values from -16 to 16
- aligned_embedding: bfloat16 [512, 64, 2048], P('pj', None, 'pi'), may hold values from -6 to 6
- aligned_scaling_weights: float32 [64], replicated, may hold values from 0.5 to 1.5
- aligned_shift_vector: float32 [64], replicated, may hold values from -3 to 3
- payload_weights: bfloat16 [64, 256], replicated, may hold values from -0.75 to 0.75
- switch_weights: bfloat16 [64, 256], replicated, may hold values from -0.75 to 0.75
- closing_weights: bfloat16 [256, 64], replicated, may hold values from -1.5 to 1.5
Outputs:
- update: bfloat16 [512, 64, 2048], P('pj', None, 'pi')
All inputs are finite; a program needn't handle non-finite values.
Results may differ from a plain program's by a relative error of at most 0.009.
Values may be sent and summed in bfloat16 or wider, within the bound.
A program may use at most 192 MiB of HBM per device.

v0:
```python
import jax
import jax.numpy as jnp
from jax import lax
from jax.sharding import Mesh
from jax.sharding import PartitionSpec as P

PI = ("pi_0", "pi_1")


EPS = 1e-05


def gathered_total(x, axis):
    return lax.all_gather(x, axis).max(0)


def over_pieces(x, axis):
    blocks = lax.all_gather(x, axis)
    return blocks.sum(axis=0)


def gathered_by_axis(x, axes, dim):
    for axis in reversed(axes):
        x = lax.all_gather(x, axis, axis=dim, tiled=True)
    return x


def rescale_embedding(inputs, axis):
    row_mean = jnp.mean(inputs, axis=axis, keepdims=True)
    centred = inputs - row_mean
    variance = jnp.mean(centred * centred, axis=axis, keepdims=True)
    return centred * lax.rsqrt(variance + EPS)


def body(
    duo_embedding,
    duo_attention_weights,
    aligned_embedding,
    aligned_scaling_weights,
    aligned_shift_vector,
    payload_weights,
    switch_weights,
    closing_weights,
):
    attender_tally = duo_attention_weights.shape[1]
    entry_tally = duo_embedding.shape[0]
    aligned_seq_tally = aligned_embedding.shape[0]
    inner_embed_size = payload_weights.shape[1]
    attender_span = inner_embed_size // attender_tally
    pair_normed = rescale_embedding(duo_embedding.astype(jnp.float32), 2)
    scores = jnp.einsum(
        "ijc,ch->hij", pair_normed, duo_attention_weights, precision=lax.Precision.HIGHEST
    )
    row_peak = gathered_total(jnp.max(scores, axis=2), "pj")
    exp_scores = jnp.exp(scores - row_peak[:, :, None]).astype(jnp.bfloat16)
    row_total = over_pieces(jnp.sum(exp_scores, axis=2, dtype=jnp.float32), "pj")
    weights_full = lax.all_gather(exp_scores, "pj", axis=2, tiled=True)
    rescaled_aligned = (
        rescale_embedding(aligned_embedding.astype(jnp.float32), 1)
        * aligned_scaling_weights[None, :, None]
        + aligned_shift_vector[None, :, None]
    ).astype(jnp.bfloat16)
    switch_share = jax.nn.sigmoid(
        jnp.einsum(
            "scn,ce->sen", rescaled_aligned, switch_weights, preferred_element_type=jnp.float32
        )
    )
    value_segment = jnp.einsum(
        "scn,ce->sen",
        gathered_by_axis(rescaled_aligned, PI, 2),
        payload_weights,
        preferred_element_type=jnp.float32,
    ).astype(jnp.bfloat16)
    piece_span = value_segment.shape[2]
    payload_each_attender = value_segment.reshape(
        aligned_seq_tally, attender_tally, attender_span, piece_span
    )
    numerator = jnp.einsum(
        "hij,shcj->shci", weights_full, payload_each_attender, preferred_element_type=jnp.float32
    )
    gate_per_head = switch_share.reshape(
        aligned_seq_tally, attender_tally, attender_span, entry_tally
    )
    averaged_result = (gate_per_head * (numerator / row_total[None, :, None, :])).astype(
        jnp.bfloat16
    )
    averaged_result = averaged_result.reshape(aligned_seq_tally, inner_embed_size, entry_tally)
    return jnp.einsum(
        "ser,ec->scr", averaged_result, closing_weights, preferred_element_type=jnp.float32
    ).astype(jnp.bfloat16)


def solution(mesh):
    finer = Mesh(mesh.devices.reshape(4, 2, mesh.shape["pj"]), ("pi_0", "pi_1", "pj"))
    placed = (P(PI, "pj", None), P(), P("pj", None, PI), P(), P(), P(), P(), P())
    return jax.shard_map(
        body, mesh=finer, in_specs=placed, out_specs=P("pj", None, PI), check_vma=False
    )
```

profile of v0, /device:TPU:1, one launch (start us, length us, event | category | flops | bytes accessed | tf_op | source)
XLA Modules:
  0.0 258.4 jit_solution(3760978803032783942)
XLA Ops:
  6.5 0.0 copy-start
  6.5 1.4 convert_reduce_fusion.1
  8.0 1.6 fusion.17
  9.6 2.7 %fusion.20 = bf16[32,64,256]{2,1,0:T(8,128)(2,1)} fusion(bf16[32,64,256]{2,1,0:T(8,128)(2,1)} %param.10, f32[64]{0:T(128)} %param.12, f32[64]{0:T(128)} %param.11, f32[32,256]{1,0:T(8,128)S(1)} %add_rsqrt_fusion.1, f32[32,256]{1,0:T(8,128)S(1)} %broadcast_multiply_fusion.1), kind=kLoop, calls=%fused_computation.22 | loop fusion | flops 3145728 | bytes 2163200 | tf_op jit(solution)/shard_map/convert_element_type | solution.py:62
  12.3 0.0 all-gather.6.cloned.1.call-update
  12.4 0.0 all-gather.8.cloned.1.call-start
  12.4 38.7 %all-gather.6.cloned.1.call-done = bf16[32,64,512]{2,1,0:T(8,128)(2,1)} async-done(((bf16[32,64,256]{2,1,0:T(8,128)(2,1)}), bf16[32,64,512]{2,1,0:T(8,128)(2,1)}) %all-gather.6.cloned.1.call-update) | async-done | bytes 2097168 | tf_op jit(solution)/shard_map/all_gather | solution.py:24
  51.1 0.0 all-gather.8.cloned.1.call-update
  51.1 0.0 copy-start.5
  51.2 0.0 all-gather.10.cloned.1.call-start
  51.2 0.0 slice-start
  51.2 5.8 %convert_reduce_fusion = f32[256,128]{1,0:T(8,128)S(1)} fusion(bf16[256,128,128]{2,1,0:T(8,128)(2,1)} %param.8), kind=kLoop, calls=%fused_computation.3 | loop fusion | flops 8355840 | bytes 8519680 | tf_op jit(solution)/shard_map/reduce_sum | solution.py:29
  57.0 0.0 slice-start.1
  57.1 10.9 %fusion.4 = f32[256,128]{1,0:T(8,128)S(1)} fusion(bf16[256,128,128]{2,1,0:T(8,128)(2,1)} %param.8, f32[256,128]{1,0:T(8,128)S(1)} %broadcast_multiply_fusion), kind=kLoop, calls=%fused_computation.7 | loop fusion | flops 16744448 | bytes 8650752 | tf_op jit(solution)/shard_map/reduce_sum | solution.py:31
  68.0 0.0 copy-done.5
  68.0 0.0 slice-done
  68.0 0.0 copy-start.2
  68.0 0.0 copy-start.4
  68.0 31.4 %fusion.29 = (f32[8,256]{0,1:T(8,128)S(1)}, f32[8,256,128]{2,0,1:T(8,128)S(1)}) fusion(f32[128,8]{0,1:T(8,128)S(1)} %copy-done.5, bf16[256,128,128]{2,1,0:T(8,128)(2,1)S(1)} %bitcast.39, f32[256,128]{1,0:T(8,128)S(1)} %add_rsqrt_fusion, f32[256,128]{1,0:T(8,128)S(1)} %broadcast_multiply_fusion), kind=kOutput, calls=%fused_computation.38 | convolution fusion | flops 415496192 | bytes 9711616 | tf_op jit(solution)/shard_map/ijc,ch->hij/dot_general | solution.py:51
  99.4 0.1 copy.26
  99.5 25.0 %all-gather = f32[128,256]{1,0:T(8,128)S(1)} all-gather(f32[8,256]{1,0:T(8,128)S(1)} %copy.26), channel_id=2, replica_groups=mesh['pi_0'=4,'pi_1'=2,'pj'=16] {'pj'}, dimensions={0}, use_global_device_ids=true | all-gather | bytes 139264 | tf_op jit(solution)/shard_map/all_gather | solution.py:14
  124.5 0.1 copy.27
  124.6 1.2 convert_reduce_fusion.2
  125.8 0.0 all-gather.10.cloned.1.call-update
  125.8 0.1 copy.30
  125.9 19.6 %all-gather.1 = f32[128,256]{1,0:T(8,128)S(1)} all-gather(f32[8,256]{1,0:T(8,128)S(1)} %copy.30), channel_id=3, replica_groups=mesh['pi_0'=4,'pi_1'=2,'pj'=16] {'pj'}, dimensions={0}, use_global_device_ids=true | all-gather | bytes 139264 | tf_op jit(solution)/shard_map/all_gather | solution.py:18
  145.6 5.9 %add_divide_fusion = f32[32,256,256]{1,2,0:T(8,128)} fusion(bf16[32,64,256]{2,1,0:T(8,128)(2,1)S(1)} %copy-done.2, bf16[64,256]{1,0:T(8,128)(2,1)S(1)} %copy-done.4), kind=kOutput, calls=%fused_computation.14 | convolution fusion | flops 274726912 | bytes 9469952 | tf_op jit(solution)/shard_map/scn,ce->sen/dot_general | solution.py:64
  151.5 17.4 %convolution_convert_fusion = bf16[32,2048,256]{1,2,0:T(8,128)(2,1)} fusion(bf16[32,64,2048]{2,1,0:T(8,128)(2,1)} %all-gather.8.cloned.1.call-done, bf16[64,256]{1,0:T(8,128)(2,1)S(1)} %copy-done), kind=kOutput, calls=%fused_computation.4 | convolution fusion | flops 2164260864 | bytes 41975808 | tf_op jit(solution)/shard_map/scn,ce->sen/dot_general | solution.py:68
  168.9 48.3 %all-gather.10.cloned.1.call-done = bf16[8,256,2048]{2,0,1:T(8,128)(2,1)} async-done(((bf16[8,256,128]{2,0,1:T(8,128)(2,1)}), bf16[8,256,2048]{2,0,1:T(8,128)(2,1)}) %all-gather.10.cloned.1.call-update) | async-done | bytes 8388624 | tf_op jit(solution)/shard_map/all_gather | solution.py:57
  217.2 30.2 %fusion.7 = bf16[32,8,32,256]{3,2,0,1:T(8,128)(2,1)} fusion(f32[32,8,32,256]{3,2,1,0:T(8,128)} %bitcast.42, bf16[8,256,2048,1]{2,0,1,3:T(8,128)(2,1)} %bitcast.41, bf16[32,8,32,2048]{3,2,1,0:T(8,128)(2,1)} %bitcast.37, f32[8,256]{1,0:T(8,128)S(1)} %bitcast_reduce_fusion), kind=kOutput, calls=%fused_computation.10 | convolution fusion | flops 8596226048 | bytes 54534144 | tf_op jit(solution)/shard_map/hij,shcj->shci/dot_general | solution.py:78
  247.4 2.6 %copy.32 = bf16[32,8,32,256]{3,2,1,0:T(8,128)(2,1)S(1)} copy(bf16[32,8,32,256]{3,2,0,1:T(8,128)(2,1)} %fusion.7) | data formatting | bytes 8388608 | tf_op jit(solution)/shard_map/convert_element_type | solution.py:84
  250.1 1.8 fusion.21
  (17 shorter events, 0.1 us)
Async XLA Ops:
  6.5 144.9 %copy-start = (bf16[64,256]{1,0:T(8,128)(2,1)S(1)}, bf16[64,256]{1,0:T(8,128)(2,1)}, u32[]{:S(2)}) copy-start(bf16[64,256]{1,0:T(8,128)(2,1)} %param.13) | copy-start | bytes 98308
  6.5 44.6 %all-gather.6.cloned.1.call-start = ((), (), s32[]{:S(2)}) async-start(), calls=%async_computation | async-start | bytes 3145728 | tf_op jit(solution)/shard_map/all_gather | solution.py:24
  12.4 139.1 %all-gather.8.cloned.1.call-start = ((), (), s32[]{:S(2)}) async-start(), calls=%async_computation.1 | async-start | bytes 10485760 | tf_op jit(solution)/shard_map/all_gather | solution.py:24
  51.1 16.8 %copy-start.5 = (f32[128,8]{0,1:T(8,128)S(1)}, f32[128,8]{0,1:T(8,128)}, u32[]{:S(2)}) copy-start(f32[128,8]{0,1:T(8,128)} %param.9) | copy-start | bytes 12292
  51.2 166.1 %all-gather.10.cloned.1.call-start = ((), (), s32[]{:S(2)}) async-start(), calls=%async_computation.2 | async-start | bytes 8912896 | tf_op jit(solution)/shard_map/all_gather | solution.py:57
  51.2 16.8 %slice-start = ((s8[8388608]{0:T(1024)(128)(4,1)}), s8[4194304]{0:T(1024)(128)(4,1)S(1)}, s32[]{:S(2)}) async-start(s8[8388608]{0:T(1024)(128)(4,1)} %bitcast.38), calls=%async_computation.3 | async-start | bytes 8388608
  57.0 10.9 %slice-start.1 = ((s8[8388608]{0:T(1024)(128)(4,1)}), s8[4194304]{0:T(1024)(128)(4,1)S(1)}, s32[]{:S(2)}) async-start(s8[8388608]{0:T(1024)(128)(4,1)} %bitcast.38), calls=%async_computation.4 | async-start | bytes 8388608
  68.0 77.5 %copy-start.2 = (bf16[32,64,256]{2,1,0:T(8,128)(2,1)S(1)}, bf16[32,64,256]{2,1,0:T(8,128)(2,1)}, u32[]{:S(2)}) copy-start(bf16[32,64,256]{2,1,0:T(8,128)(2,1)} %fusion.20) | copy-start | bytes 3145732
  68.0 77.5 %copy-start.4 = (bf16[64,256]{1,0:T(8,128)(2,1)S(1)}, bf16[64,256]{1,0:T(8,128)(2,1)}, u32[]{:S(2)}) copy-start(bf16[64,256]{1,0:T(8,128)(2,1)} %param.14) | copy-start | bytes 98308
  217.2 34.7 %copy-start.1 = (bf16[64,256]{1,0:T(8,128)(2,1)S(1)}, bf16[64,256]{1,0:T(8,128)(2,1)}, u32[]{:S(2)}) copy-start(bf16[64,256]{1,0:T(8,128)(2,1)} %param.13) | copy-start | bytes 98308
  247.4 2.6 %copy-start.3 = (bf16[256,64]{0,1:T(8,128)(2,1)S(1)}, bf16[256,64]{0,1:T(8,128)(2,1)}, u32[]{:S(2)}) copy-start(bf16[256,64]{0,1:T(8,128)(2,1)} %param.15) | copy-start | bytes 98308
Sparse Core Ops, SparseCore 0:
  12.5 38.5 all-gather.5
  52.8 84.0 all-gather.7
  139.2 78.0 all-gather.9
where the time goes:
time: 259 us; the launch traced here: 258 us
  waiting for transfers between devices  87.1 us (34%)
  matrix products  86.8 us (34%)
  blocking collectives  44.6 us (17%)
  other arithmetic  23.7 us (9%)
  between operations  13.3 us (5%)
  local copies, waits for them, and re-layouts  2.92 us (1%)
    all_gather x1, waiting for transfers between devices, body(): weights_full = lax.all_gather(exp_scores, 'pj', axis=2, tiled=True)  48.3 us
    all_gather x2, waiting for transfers between devices, gathered_by_axis(): x = lax.all_gather(x, axis, axis=dim, tiled=True)  38.7 us
    dot_general x1, matrix products, body(): jnp.einsum('ijc,ch->hij', pair_normed, duo_attention_weights, precision=l...  31.4 us
    dot_general x1, matrix products, body(): jnp.einsum('hij,shcj->shci', weights_full, payload_each_attender, preferr...  30.2 us
    all_gather x1, blocking collectives, gathered_total(): return lax.all_gather(x, axis).max(0)  25 us
    all_gather x1, blocking collectives, over_pieces(): blocks = lax.all_gather(x, axis)  19.6 us
    dot_general x1, matrix products, body(): jnp.einsum('scn,ce->sen', gathered_by_axis(rescaled_aligned, PI, 2), payl...  17.4 us
    reduce_sum x2, other arithmetic, rescale_embedding(): variance = jnp.mean(centred * centred, axis=axis, keepdims=True)  12.5 us
  transfers between devices with their start and end apart: 3, of which 2 were waited for; matrix products, arithmetic and copies ran while one was open for 28% of the time, Pallas kernels for 0%

commit v1 on v0

v1 whole, which is shorter than its diff:
```python
import functools

import jax
import jax.numpy as jnp
from jax import lax
from jax.experimental import pallas as pl
from jax.experimental.pallas import tpu as pltpu
from jax.sharding import PartitionSpec as P

EPS = 1e-05
F32 = jnp.float32
BF16 = jnp.bfloat16
MESH = pl.DeviceIdType.MESH
NT = (((1,), (1,)), ((), ()))

HEADS = 8
SPAN = 32
ROWS = 32
CH = 64
TOK = 256
X_ROWS = 24
NPIECES = 8


def kernel(
    duo_hbm, wt_ref, msa_ref, gain_ref, shift_ref, pw_ref, sw_ref, cw_ref,
    out_ref,
    nbuf, ebuf, duo, sc, st, mx, acc, gate, vbuf, tot, pwt, swt, cwt, gcol,
    duo_sem, n_send, n_recv, e_send, e_recv, m_send, m_recv,
):
    pi = lax.axis_index("pi")
    pj = lax.axis_index("pj")
    y, xl = lax.div(pi, 2), lax.rem(pi, 2)
    xh, zc = lax.div(pj, 8), lax.rem(pj, 8)
    z, core = lax.div(zc, 2), lax.rem(zc, 2)

    def pi_of(yy, ll):
        return yy * 2 + ll

    def pj_of(hh, zz, cc):
        return hh * 8 + zz * 2 + cc

    yp, ym, yo = lax.rem(y + 1, 4), lax.rem(y + 3, 4), lax.rem(y + 2, 4)
    zp, zm, zo = lax.rem(z + 1, 4), lax.rem(z + 3, 4), lax.rem(z + 2, 4)
    ol, oh = 1 - xl, 1 - xh

    step = 256 // NPIECES

    def duo_copy(k):
        rows = pl.ds(k * step, step)
        return pltpu.make_async_copy(duo_hbm.at[rows], duo.at[rows], duo_sem.at[k])

    for k in range(NPIECES):
        duo_copy(k).start()

    barrier = pltpu.get_barrier_semaphore()
    for d in range(1, 16):
        pl.semaphore_signal(
            barrier, inc=1, device_id={"pi": pi, "pj": lax.rem(pj + d, 16)}, device_id_type=MESH
        )
    for other in (pi_of(yp, xl), pi_of(ym, xl), pi_of(y, ol)):
        pl.semaphore_signal(
            barrier, inc=1, device_id={"pi": other, "pj": pj}, device_id_type=MESH
        )

    def column(ref):
        row = jnp.broadcast_to(ref[...], (CH, CH))
        r = lax.broadcasted_iota(jnp.int32, (CH, CH), 0)
        c = lax.broadcasted_iota(jnp.int32, (CH, CH), 1)
        col = jnp.sum(jnp.where(r == c, row, 0.0), axis=1, keepdims=True)
        return jnp.broadcast_to(col, (CH, TOK))

    gcol[0] = column(gain_ref)
    gcol[1] = column(shift_ref)

    def norm_row(s, _):
        v = msa_ref[s].astype(F32)
        mean = jnp.mean(v, axis=0, keepdims=True)
        v = v - mean
        var = jnp.mean(v * v, axis=0, keepdims=True)
        v = v * lax.rsqrt(var + EPS)
        nbuf[pi, s] = (v * gcol[0] + gcol[1]).astype(BF16)
        return 0

    lax.fori_loop(0, ROWS, norm_row, 0)
    pl.semaphore_wait(barrier, 18)

    xa, xb = X_ROWS // 2, X_ROWS
    ya, yb = X_ROWS + (ROWS - X_ROWS) // 2, ROWS

    def n_copy(k, block, lo, hi, to_y, to_l):
        view = nbuf.at[block, pl.ds(lo, hi - lo)]
        return pltpu.make_async_remote_copy(
            src_ref=view, dst_ref=view, send_sem=n_send.at[k], recv_sem=n_recv.at[k],
            device_id={"pi": pi_of(to_y, to_l), "pj": pj}, device_id_type=MESH,
        )

    own, part = pi, pi_of(y, ol)
    b_m, b_p, b_o = pi_of(ym, xl), pi_of(yp, xl), pi_of(yo, xl)
    q_m, q_p = pi_of(ym, ol), pi_of(yp, ol)
    n = [
        n_copy(0, own, 0, xb, y, ol),
        n_copy(1, own, xb, yb, y, ol),
        n_copy(2, own, xb, yb, yp, xl),
        n_copy(3, own, 0, xb, yp, xl),
        n_copy(4, own, xb, yb, ym, xl),
        n_copy(5, own, 0, xb, ym, xl),
        n_copy(6, b_m, xb, ya, yp, xl),
        n_copy(7, b_p, ya, yb, ym, xl),
        n_copy(8, b_m, xb, yb, y, ol),
        n_copy(9, b_p, xb, yb, y, ol),
        n_copy(10, b_o, xb, ya, y, ol),
        n_copy(11, b_o, ya, yb, y, ol),
        n_copy(12, part, 0, xb, yp, xl),
        n_copy(13, part, 0, xb, ym, xl),
        n_copy(14, b_m, 0, xa, yp, xl),
        n_copy(15, b_p, xa, xb, ym, xl),
        n_copy(16, q_m, 0, xa, yp, xl),
        n_copy(17, q_p, xa, xb, ym, xl),
    ]
    for k in (2, 4, 0, 3, 5):
        n[k].start()

    pwt[...] = pw_ref[...].astype(F32).T.astype(BF16)
    swt[...] = sw_ref[...].astype(F32).T.astype(BF16)
    cwt[...] = cw_ref[...].astype(F32).T.astype(BF16)

    w = wt_ref[...]
    w = w - jnp.mean(w, axis=1, keepdims=True)
    w_sum = jnp.sum(w, axis=1, keepdims=True)
    w_hi = w.astype(BF16)
    w_rest = w - w_hi.astype(F32)
    w_mid = w_rest.astype(BF16)
    w_lo = (w_rest - w_mid.astype(F32)).astype(BF16)
    ones8 = jnp.ones((8, 128), F32)
    stack = jnp.concatenate(
        [w_hi.astype(F32), w_mid.astype(F32), w_lo.astype(F32), ones8], axis=0
    ).astype(BF16)
    ones = jnp.ones((16, 128), BF16)
    group = 16

    def score_group(g, _):
        i0 = g * group
        x = duo[pl.ds(i0, group)].reshape(group * 128, 128)
        xf = x.astype(F32)
        sq = xf * xf
        sq_hi = sq.astype(BF16)
        sq_lo = (sq - sq_hi.astype(F32)).astype(BF16)
        r = lax.dot_general(stack, x, NT, preferred_element_type=F32)
        t_hi = lax.dot_general(ones, sq_hi, NT, preferred_element_type=F32)[0:8]
        t_lo = lax.dot_general(ones, sq_lo, NT, preferred_element_type=F32)[0:8]
        mean = r[24:32] * (1.0 / 128)
        m_hi = mean.astype(BF16).astype(F32)
        m_lo = mean - m_hi
        var = t_hi * (1.0 / 128) - m_hi * m_hi
        var = var - 2.0 * m_hi * m_lo
        var = (var - m_lo * m_lo) + t_lo * (1.0 / 128)
        var = jnp.maximum(var, 0.0)
        dots = (r[16:24] + r[8:16]) + r[0:8]
        s = (dots - mean * w_sum) * lax.rsqrt(var + EPS)
        for a in range(group):
            rows = pl.ds(pl.multiple_of((i0 + a) * 8, 8), 8)
            sc[rows, :] = s[:, a * 128:(a + 1) * 128]
        return 0

    per = step // group

    def score_piece(k, _):
        duo_copy(k).wait()
        lax.fori_loop(k * per, (k + 1) * per, score_group, 0)
        return 0

    lax.fori_loop(0, NPIECES, score_piece, 0)

    for h in range(HEADS):
        t = sc[pl.ds(h, 256, stride=8), :].T
        st[h] = t
        mx[pj, pl.ds(h, 1), :] = jnp.max(t, axis=0, keepdims=True)

    def m_copy(d):
        return pltpu.make_async_remote_copy(
            src_ref=mx.at[pj], dst_ref=mx.at[pj], send_sem=m_send.at[d - 1],
            recv_sem=m_recv.at[d - 1],
            device_id={"pi": pi, "pj": lax.rem(pj + d, 16)}, device_id_type=MESH,
        )

    for d in range(1, 16):
        m_copy(d).start()

    n[2].wait_recv()
    n[6].start()
    n[4].wait_recv()
    n[7].start()

    def gate_row(s, _):
        g = jnp.dot(swt[...], nbuf[pi, s], preferred_element_type=F32)
        gate[s] = jax.nn.sigmoid(g)
        return 0

    lax.fori_loop(0, ROWS, gate_row, 0)

    for d in range(1, 16):
        m_copy(d).wait_recv()
    peak = mx[0]
    for d in range(1, 16):
        peak = jnp.maximum(peak, mx[d])
    mx_peak = peak

    block = xh * 4 + z
    half = pl.ds(pl.multiple_of(core * 128, 128), 128)
    for h in range(HEADS):
        ebuf[block, h, half, :] = jnp.exp(st[h] - mx_peak[h:h + 1]).astype(BF16)

    def e_copy(k, hh, zz, h0, h1, to_h, to_z, to_c):
        view = ebuf.at[hh * 4 + zz, pl.ds(h0, h1 - h0), half]
        return pltpu.make_async_remote_copy(
            src_ref=view, dst_ref=view, send_sem=e_send.at[k], recv_sem=e_recv.at[k],
            device_id={"pi": pi, "pj": pj_of(to_h, to_z, to_c)}, device_id_type=MESH,
        )

    oc = 1 - core
    e = [
        e_copy(0, xh, z, 0, 8, xh, z, oc),
        e_copy(1, xh, z, 0, 8, oh, z, core),
        e_copy(2, xh, z, 0, 8, xh, zp, core),
        e_copy(3, xh, z, 0, 8, xh, zm, core),
        e_copy(4, oh, z, 0, 8, xh, zp, core),
        e_copy(5, oh, z, 0, 8, xh, zm, core),
        e_copy(6, oh, z, 0, 8, xh, z, oc),
        e_copy(7, xh, zm, 0, 4, xh, zp, core),
        e_copy(8, xh, zm, 0, 8, xh, z, oc),
        e_copy(9, xh, zp, 4, 8, xh, zm, core),
        e_copy(10, xh, zp, 0, 8, xh, z, oc),
        e_copy(11, xh, zo, 0, 4, xh, z, oc),
        e_copy(12, xh, zo, 4, 8, xh, z, oc),
        e_copy(13, oh, zm, 0, 4, xh, zp, core),
        e_copy(14, oh, zm, 0, 8, xh, z, oc),
        e_copy(15, oh, zp, 4, 8, xh, zm, core),
        e_copy(16, oh, zp, 0, 8, xh, z, oc),
        e_copy(17, oh, zo, 0, 4, xh, z, oc),
        e_copy(18, oh, zo, 4, 8, xh, z, oc),
    ]
    for k in (1, 2, 3, 0):
        e[k].start()
    for k in (1, 8, 9):
        n[k].start()

    acc[...] = jnp.zeros_like(acc)
    tot[...] = jnp.zeros_like(tot)

    n[0].wait_recv()
    n[12].start()
    n[13].start()
    n[3].wait_recv()
    n[14].start()
    n[5].wait_recv()
    n[15].start()
    n[6].wait_recv()
    n[10].start()
    n[7].wait_recv()
    n[11].start()
    e[2].wait_recv()
    e[7].start()
    e[8].start()
    e[3].wait_recv()
    e[9].start()
    e[10].start()
    e[1].wait_recv()
    for k in (4, 5, 6):
        e[k].start()
    e[7].wait_recv()
    e[11].start()
    e[9].wait_recv()
    e[12].start()
    n[12].wait_recv()
    n[16].start()
    n[13].wait_recv()
    n[17].start()
    e[4].wait_recv()
    e[13].start()
    e[14].start()
    e[5].wait_recv()
    e[15].start()
    e[16].start()
    e[13].wait_recv()
    e[17].start()
    e[15].wait_recv()
    e[18].start()
    for k in (0, 8, 10, 11, 12, 6, 14, 16, 17, 18):
        e[k].wait_recv()

    ones_t = jnp.ones((16, TOK), BF16)

    def value_row(p, s, _):
        v = jnp.dot(pwt[...], nbuf[p, s], preferred_element_type=F32)
        vbuf[s] = v.astype(BF16)
        return 0

    def head_step(p, h, _):
        rows = pl.ds(pl.multiple_of(h * SPAN, SPAN), SPAN)
        weights = ebuf[p, h]
        v = vbuf[:, rows, :].reshape(ROWS * SPAN, TOK)
        part_sum = jnp.dot(v, weights, preferred_element_type=F32)
        acc[:, rows, :] += part_sum.reshape(ROWS, SPAN, TOK)
        tot[h] += jnp.dot(ones_t, weights, preferred_element_type=F32)[0:8]
        return 0

    def one_block(p):
        lax.fori_loop(0, ROWS, functools.partial(value_row, p), 0)
        lax.fori_loop(0, HEADS, functools.partial(head_step, p), 0)

    one_block(own)
    one_block(b_m)
    one_block(b_p)
    n[1].wait_recv()
    one_block(part)
    n[8].wait_recv()
    one_block(q_m)
    n[9].wait_recv()
    one_block(q_p)
    n[14].wait_recv()
    n[15].wait_recv()
    one_block(b_o)
    for k in (10, 11, 16, 17):
        n[k].wait_recv()
    one_block(pi_of(yo, ol))

    for h in range(HEADS):
        tot[h] = 1.0 / tot[h]

    def out_row(s, _):
        pieces = []
        for h in range(HEADS):
            rows = slice(h * SPAN, (h + 1) * SPAN)
            share = tot[h, 0:1, :]
            pieces.append((gate[s, rows, :] * (acc[s, rows, :] * share)).astype(BF16))
        mixed = jnp.concatenate(pieces, axis=0)
        out_ref[s] = jnp.dot(cwt[...], mixed, preferred_element_type=F32).astype(BF16)
        return 0

    lax.fori_loop(0, ROWS, out_row, 0)

    for c in n + e:
        c.wait_send()
    for d in range(1, 16):
        m_copy(d).wait_send()


def body(duo, w, msa, gain, shift, pw, sw, cw):
    vm = pl.BlockSpec(memory_space=pltpu.VMEM)
    return pl.pallas_call(
        kernel,
        out_shape=jax.ShapeDtypeStruct((ROWS, CH, TOK), BF16),
        in_specs=[pl.BlockSpec(memory_space=pl.ANY)] + [vm] * 7,
        out_specs=vm,
        scratch_shapes=[
            pltpu.VMEM((8, ROWS, CH, TOK), BF16),
            pltpu.VMEM((8, HEADS, TOK, TOK), BF16),
            pltpu.VMEM((256, 128, 128), BF16),
            pltpu.VMEM((256 * HEADS, 128), F32),
            pltpu.VMEM((HEADS, 128, TOK), F32),
            pltpu.VMEM((16, HEADS, TOK), F32),
            pltpu.VMEM((ROWS, 256, TOK), F32),
            pltpu.VMEM((ROWS, 256, TOK), F32),
            pltpu.VMEM((ROWS, 256, TOK), BF16),
            pltpu.VMEM((HEADS, 8, TOK), F32),
            pltpu.VMEM((256, CH), BF16),
            pltpu.VMEM((256, CH), BF16),
            pltpu.VMEM((CH, 256), BF16),
            pltpu.VMEM((2, CH, TOK), F32),
            pltpu.SemaphoreType.DMA((NPIECES,)),
            pltpu.SemaphoreType.DMA((18,)),
            pltpu.SemaphoreType.DMA((18,)),
            pltpu.SemaphoreType.DMA((19,)),
            pltpu.SemaphoreType.DMA((19,)),
            pltpu.SemaphoreType.DMA((15,)),
            pltpu.SemaphoreType.DMA((15,)),
        ],
        compiler_params=pltpu.CompilerParams(
            collective_id=0, has_side_effects=True, vmem_limit_bytes=66_000_000
        ),
        name="pair_average",
    )(duo, w.T, msa, gain.reshape(1, CH), shift.reshape(1, CH), pw, sw, cw)


def solution(mesh):
    placed = (P("pi", "pj", None), P(), P("pj", None, "pi"), P(), P(), P(), P(), P())
    return jax.shard_map(
        body, mesh=mesh, in_specs=placed, out_specs=P("pj", None, "pi"), check_vma=False
    )
```

time: 259 us -> 144 us (0.56)
  Pallas kernels: 0 us -> 140 us
  waiting for transfers between devices: 87.1 us -> 0 us
  matrix products: 86.8 us -> 0 us
  blocking collectives: 44.6 us -> 0 us
  other arithmetic: 23.7 us -> 0 us
  between operations: 13.3 us -> 0.01 us
    pallas_call x0 -> x1, Pallas kernels: none -> 140 us  [body(): pl.pallas_call(kernel, out_shape=jax.ShapeDtypeStruct((ROWS, CH, TOK), BF...]
    all_gather x3 -> x0, waiting for transfers between devices: 87 us -> none  [the longest x1 48.3 us: body(): weights_full = lax.all_gather(exp_scores, 'pj', axis=2, tiled=True)]
    dot_general x5 -> x0, matrix products: 86.8 us -> none  [the longest x1 31.4 us: body(): jnp.einsum('ijc,ch->hij', pair_normed, duo_attention_weights, precision=l...]
    all_gather x2 -> x0, blocking collectives: 44.6 us -> none  [the longest x1 25 us: gathered_total(): return lax.all_gather(x, axis).max(0)]
    reduce_sum x6 -> x0, other arithmetic: 20.9 us -> none  [the longest x2 12.5 us: rescale_embedding(): variance = jnp.mean(centred * centred, axis=axis, keepdims=True)]
    unnamed x16 -> x2, local copies, waits for them, and re-layouts: 0.05 us -> 3.79 us
    convert_element_type x1 -> x0, other arithmetic: 2.72 us -> none  [body(): rescaled_aligned = (rescale_embedding(aligned_embedding.astype(jnp.float3...]
    convert_element_type x1 -> x0, local copies, waits for them, and re-layouts: 2.63 us -> none  [body(): (gate_per_head * (numerator / row_total[None, :, None, :])).astype(jnp.bf...]
  transfers between devices with their start and end apart: 3 -> 0, of which waited for: 2 -> 0; matrix products, arithmetic and copies ran while one was open for 28% -> 0% of each run, Pallas kernels for 0% -> 0%
where the time goes in v1:
time: 144 us
  Pallas kernels  140 us (97%)
  local copies, waits for them, and re-layouts  3.79 us (3%)
    pallas_call x1, Pallas kernels, body(): pl.pallas_call(kernel, out_shape=jax.ShapeDtypeStruct((ROWS, CH, TOK), BF...  140 us
    unnamed x2, local copies, waits for them, and re-layouts  3.79 us

profile of v1, /device:TPU:1, one launch (start us, length us, event | category | flops | bytes accessed | tf_op | source)
XLA Modules:
  0.0 144.1 jit_solution(2076649542430780547)
XLA Ops:
  0.0 1.5 %copy.9.cw_ref = bf16[256,64]{1,0:T(8,128)(2,1)} copy(bf16[256,64]{0,1:T(8,128)(2,1)} %param.15) | data formatting | bytes 65536 | tf_op args[7]
  1.5 140.3 %pair_average.1 = bf16[32,64,256]{2,1,0:T(8,128)(2,1)} custom-call(bf16[256,128,128]{2,1,0:T(8,128)(2,1)} %duo_hbm.1, f32[8,128]{1,0:T(8,128)} %bitcast.3, bf16[32,64,256]{2,1,0:T(8,128)(2,1)} %msa_ref.1, f32[1,64]{1,0:T(1,128)} %bitcast.4, f32[1,64]{1,0:T(1,128)} %bitcast.5, bf16[64,256]{1,0:T(8,128)(2,1)} %pw_ref.1, bf16[64,256]{1,0:T(8,128)(2,1)} %sw_ref.1, ...), custom_call_target="tpu_custom_call" | custom-call | tf_op jit(solution)/shard_map/pair_average/pallas_call | solution.py:351
  141.8 2.3 %copy.11 = bf16[32,64,256]{2,1,0:T(8,128)(2,1)} copy(bf16[32,64,256]{2,1,0:T(8,128)(2,1)} %pair_average.1) | data formatting | bytes 2097152

commit v2 on v1

v2 whole, which is shorter than its diff:
```python
import functools

import jax
import jax.numpy as jnp
from jax import lax
from jax.experimental import pallas as pl
from jax.experimental.pallas import tpu as pltpu
from jax.sharding import PartitionSpec as P

EPS = 1e-05
F32 = jnp.float32
BF16 = jnp.bfloat16
MESH = pl.DeviceIdType.MESH
NT = (((1,), (1,)), ((), ()))

HEADS = 8
SPAN = 32
ROWS = 32
CH = 64
TOK = 256
X_ROWS = 22
NPIECES = 8


def kernel(
    duo_hbm, wt_ref, msa_ref, gain_ref, shift_ref, pw_ref, sw_ref, cw_ref,
    out_ref,
    nbuf, ebuf, sc, mx, acc, gate, vbuf, tot, pwt, swt, gcol,
    duo_sem, n_send, n_recv, e_send, e_recv, m_send, m_recv,
):
    pi = lax.axis_index("pi")
    pj = lax.axis_index("pj")
    y, xl = lax.div(pi, 2), lax.rem(pi, 2)
    xh, zc = lax.div(pj, 8), lax.rem(pj, 8)
    z, core = lax.div(zc, 2), lax.rem(zc, 2)

    def pi_of(yy, ll):
        return yy * 2 + ll

    def pj_of(hh, zz, cc):
        return hh * 8 + zz * 2 + cc

    yp, ym, yo = lax.rem(y + 1, 4), lax.rem(y + 3, 4), lax.rem(y + 2, 4)
    zp, zm, zo = lax.rem(z + 1, 4), lax.rem(z + 3, 4), lax.rem(z + 2, 4)
    ol, oh = 1 - xl, 1 - xh

    step = 128 // NPIECES

    def duo_copy(k):
        rows = pl.ds(k * step, step)
        there = pl.ds(256 + k * step, step)
        return pltpu.make_async_copy(duo_hbm.at[rows], vbuf.at[there], duo_sem.at[k])

    for k in range(NPIECES):
        duo_copy(k).start()

    barrier = pltpu.get_barrier_semaphore()
    for d in range(1, 16):
        pl.semaphore_signal(
            barrier, inc=1, device_id={"pi": pi, "pj": lax.rem(pj + d, 16)}, device_id_type=MESH
        )
    for other in (pi_of(yp, xl), pi_of(ym, xl), pi_of(y, ol)):
        pl.semaphore_signal(
            barrier, inc=1, device_id={"pi": other, "pj": pj}, device_id_type=MESH
        )

    def column(ref):
        row = jnp.broadcast_to(ref[...], (CH, CH))
        r = lax.broadcasted_iota(jnp.int32, (CH, CH), 0)
        c = lax.broadcasted_iota(jnp.int32, (CH, CH), 1)
        col = jnp.sum(jnp.where(r == c, row, 0.0), axis=1, keepdims=True)
        return jnp.broadcast_to(col, (CH, TOK))

    gcol[0] = column(gain_ref)
    gcol[1] = column(shift_ref)

    def norm_rows(g, _):
        for a in range(4):
            s = g * 4 + a
            v = msa_ref[s].astype(F32)
            mean = jnp.mean(v, axis=0, keepdims=True)
            v = v - mean
            var = jnp.mean(v * v, axis=0, keepdims=True)
            v = v * lax.rsqrt(var + EPS)
            nbuf[pi, s] = (v * gcol[0] + gcol[1]).astype(BF16)
        return 0

    lax.fori_loop(0, ROWS // 4, norm_rows, 0)
    pl.semaphore_wait(barrier, 18)

    xa, xb = X_ROWS // 2, X_ROWS
    ya, yb = X_ROWS + (ROWS - X_ROWS) // 2, ROWS

    def n_copy(k, block, lo, hi, to_y, to_l):
        view = nbuf.at[block, pl.ds(lo, hi - lo)]
        return pltpu.make_async_remote_copy(
            src_ref=view, dst_ref=view, send_sem=n_send.at[k], recv_sem=n_recv.at[k],
            device_id={"pi": pi_of(to_y, to_l), "pj": pj}, device_id_type=MESH,
        )

    own, part = pi, pi_of(y, ol)
    b_m, b_p, b_o = pi_of(ym, xl), pi_of(yp, xl), pi_of(yo, xl)
    q_m, q_p = pi_of(ym, ol), pi_of(yp, ol)
    n = [
        n_copy(0, own, 0, xb, y, ol),
        n_copy(1, own, xb, yb, y, ol),
        n_copy(2, own, xb, yb, yp, xl),
        n_copy(3, own, 0, xb, yp, xl),
        n_copy(4, own, xb, yb, ym, xl),
        n_copy(5, own, 0, xb, ym, xl),
        n_copy(6, b_m, xb, ya, yp, xl),
        n_copy(7, b_p, ya, yb, ym, xl),
        n_copy(8, b_m, xb, yb, y, ol),
        n_copy(9, b_p, xb, yb, y, ol),
        n_copy(10, b_o, xb, ya, y, ol),
        n_copy(11, b_o, ya, yb, y, ol),
        n_copy(12, part, 0, xb, yp, xl),
        n_copy(13, part, 0, xb, ym, xl),
        n_copy(14, b_m, 0, xa, yp, xl),
        n_copy(15, b_p, xa, xb, ym, xl),
        n_copy(16, q_m, 0, xa, yp, xl),
        n_copy(17, q_p, xa, xb, ym, xl),
    ]
    for k in (2, 4, 0, 3, 5):
        n[k].start()

    pwt[...] = pw_ref[...].astype(F32).T.astype(BF16)
    swt[...] = sw_ref[...].astype(F32).T.astype(BF16)

    w = wt_ref[...]
    w = w - jnp.mean(w, axis=1, keepdims=True)
    w_sum = jnp.sum(w, axis=1, keepdims=True)
    w_hi = w.astype(BF16)
    w_rest = w - w_hi.astype(F32)
    w_mid = w_rest.astype(BF16)
    w_lo = (w_rest - w_mid.astype(F32)).astype(BF16)
    ones8 = jnp.ones((8, 128), F32)
    stack = jnp.concatenate(
        [w_hi.astype(F32), w_mid.astype(F32), w_lo.astype(F32), ones8], axis=0
    ).astype(BF16)
    ones = jnp.ones((16, 128), BF16)
    group = 16

    def score_group(g, _):
        x = vbuf[pl.ds(256 + g * (group // 2), group // 2)].reshape(group * 128, 128)
        xf = x.astype(F32)
        sq = xf * xf
        sq_hi = sq.astype(BF16)
        sq_lo = (sq - sq_hi.astype(F32)).astype(BF16)
        r = lax.dot_general(stack, x, NT, preferred_element_type=F32)
        t_hi = lax.dot_general(ones, sq_hi, NT, preferred_element_type=F32)[0:8]
        t_lo = lax.dot_general(ones, sq_lo, NT, preferred_element_type=F32)[0:8]
        mean = r[24:32] * (1.0 / 128)
        m_hi = mean.astype(BF16).astype(F32)
        m_lo = mean - m_hi
        var = t_hi * (1.0 / 128) - m_hi * m_hi
        var = var - 2.0 * m_hi * m_lo
        var = (var - m_lo * m_lo) + t_lo * (1.0 / 128)
        var = jnp.maximum(var, 0.0)
        dots = (r[16:24] + r[8:16]) + r[0:8]
        s = (dots - mean * w_sum) * lax.rsqrt(var + EPS)
        for a in range(group):
            rows = pl.ds(pl.multiple_of((g * group + a) * 8, 8), 8)
            sc[rows, :] = s[:, a * 128:(a + 1) * 128]
        return 0

    per = 2 * step // group

    def score_piece(k, _):
        duo_copy(k).wait()
        lax.fori_loop(k * per, (k + 1) * per, score_group, 0)
        return 0

    def m_copy(r, d):
        view = mx.at[r, pj]
        return pltpu.make_async_remote_copy(
            src_ref=view, dst_ref=view, send_sem=m_send.at[r, d - 1],
            recv_sem=m_recv.at[r, d - 1],
            device_id={"pi": pi, "pj": lax.rem(pj + d, 16)}, device_id_type=MESH,
        )

    def scores_of(r):
        lax.fori_loop(r * NPIECES // 2, (r + 1) * NPIECES // 2, score_piece, 0)
        for h in range(HEADS):
            t = sc[pl.ds(r * 1024 + h, 128, stride=8), :].T
            acc[8 + h, 0:128, r * 128:(r + 1) * 128] = t
            mx[r, pj, pl.ds(h, 1), :] = jnp.max(t, axis=0, keepdims=True)
        for d in range(1, 16):
            m_copy(r, d).start()

    def columns(zz, cc):
        return pl.ds(pl.multiple_of(lax.rem(zz, 2) * 256 + cc * 128, 128), 128)

    def pair_of(hh, zz):
        return hh * 2 + lax.div(zz, 2)

    def exps_of(r):
        for d in range(1, 16):
            m_copy(r, d).wait_recv()
        peak = mx[r, 0]
        for d in range(1, 16):
            peak = jnp.maximum(peak, mx[r, d])
        lanes = slice(r * 128, (r + 1) * 128)
        for h in range(HEADS):
            t = jnp.exp(acc[8 + h, 0:128, lanes] - peak[h:h + 1])
            ebuf[pair_of(xh, z), h, columns(z, core), lanes] = t.astype(BF16)

    def e_copy(r, k, hh, zz, h0, h1, to_h, to_z, to_c):
        view = ebuf.at[
            pair_of(hh, zz), pl.ds(h0, h1 - h0), columns(zz, core), pl.ds(r * 128, 128)
        ]
        return pltpu.make_async_remote_copy(
            src_ref=view, dst_ref=view, send_sem=e_send.at[r, k], recv_sem=e_recv.at[r, k],
            device_id={"pi": pi, "pj": pj_of(to_h, to_z, to_c)}, device_id_type=MESH,
        )

    oc = 1 - core
    e = [
        [
            e_copy(r, 0, xh, z, 0, 8, xh, z, oc),
            e_copy(r, 1, xh, z, 0, 8, oh, z, core),
            e_copy(r, 2, xh, z, 0, 8, xh, zp, core),
            e_copy(r, 3, xh, z, 0, 8, xh, zm, core),
            e_copy(r, 4, oh, z, 0, 8, xh, zp, core),
            e_copy(r, 5, oh, z, 0, 8, xh, zm, core),
            e_copy(r, 6, oh, z, 0, 8, xh, z, oc),
            e_copy(r, 7, xh, zm, 0, 4, xh, zp, core),
            e_copy(r, 8, xh, zm, 0, 8, xh, z, oc),
            e_copy(r, 9, xh, zp, 4, 8, xh, zm, core),
            e_copy(r, 10, xh, zp, 0, 8, xh, z, oc),
            e_copy(r, 11, xh, zo, 0, 4, xh, z, oc),
            e_copy(r, 12, xh, zo, 4, 8, xh, z, oc),
            e_copy(r, 13, oh, zm, 0, 4, xh, zp, core),
            e_copy(r, 14, oh, zm, 0, 8, xh, z, oc),
            e_copy(r, 15, oh, zp, 4, 8, xh, zm, core),
            e_copy(r, 16, oh, zp, 0, 8, xh, z, oc),
            e_copy(r, 17, oh, zo, 0, 4, xh, z, oc),
            e_copy(r, 18, oh, zo, 4, 8, xh, z, oc),
        ]
        for r in range(2)
    ]

    scores_of(0)
    scores_of(1)
    n[2].wait_recv()
    n[6].start()
    n[4].wait_recv()
    n[7].start()
    for r in range(2):
        exps_of(r)
        for k in (2, 3, 1, 0):
            e[r][k].start()
    for k in (1, 8, 9):
        n[k].start()

    acc[...] = jnp.zeros_like(acc)
    tot[...] = jnp.zeros_like(tot)

    def gate_rows(g, _):
        for a in range(4):
            s = g * 4 + a
            t = jnp.dot(swt[...], nbuf[pi, s], preferred_element_type=F32)
            gate[s] = jax.nn.sigmoid(t)
        return 0

    ones_t = jnp.ones((16, 2 * TOK), BF16)

    def value_rows(p, slot, c, g, _):
        for a in range(8):
            s = g * 8 + a
            v = jnp.dot(pwt[...], nbuf[p, s], preferred_element_type=F32).astype(BF16)
            vbuf[slot * 128 + s * 4 + c * 2] = v[:, 0:128]
            vbuf[slot * 128 + s * 4 + c * 2 + 1] = v[:, 128:256]
        return 0

    def head_step(yy, slot, g, _):
        v4 = vbuf.at[pl.ds(slot * 128, 128)]
        for a in range(2):
            h = g * 2 + a
            rows = pl.ds(pl.multiple_of(h * SPAN, SPAN), SPAN)
            weights = ebuf[yy, h]
            v = v4[:, rows, :].reshape(ROWS, 4, SPAN, 128)
            v = jnp.concatenate(
                [v[:, t].reshape(ROWS * SPAN, 128) for t in range(4)], axis=1
            )
            part_sum = jnp.dot(v, weights, preferred_element_type=F32)
            acc[:, rows, :] += part_sum.reshape(ROWS, SPAN, TOK)
            tot[h] += jnp.dot(ones_t, weights, preferred_element_type=F32)[0:8]
        return 0

    def values_of(p, slot, c):
        lax.fori_loop(0, ROWS // 8, functools.partial(value_rows, p, slot, c), 0)

    def product_of(yy, slot):
        lax.fori_loop(0, HEADS // 2, functools.partial(head_step, yy, slot), 0)

    lax.fori_loop(0, ROWS // 4, gate_rows, 0)
    values_of(own, 0, xl)

    def hop(k, *then):
        for r in range(2):
            e[r][k].wait_recv()
            for t in then:
                e[r][t].start()

    n[0].wait_recv()
    n[12].start()
    n[13].start()
    hop(2, 7, 8)
    hop(3, 9, 10)
    n[3].wait_recv()
    n[14].start()
    n[5].wait_recv()
    n[15].start()
    n[6].wait_recv()
    n[10].start()
    n[7].wait_recv()
    n[11].start()
    hop(1, 4, 5, 6)
    values_of(b_m, 1, xl)
    hop(7, 11)
    hop(9, 12)
    values_of(b_p, 2, xl)
    n[1].wait_recv()
    values_of(part, 0, ol)
    hop(4, 13, 14)
    hop(5, 15, 16)
    n[12].wait_recv()
    n[16].start()
    n[13].wait_recv()
    n[17].start()
    n[8].wait_recv()
    values_of(q_m, 1, ol)
    n[9].wait_recv()
    values_of(q_p, 2, ol)
    hop(13, 17)
    hop(15, 18)
    for k in (0, 8, 10, 11, 12, 6, 14, 16, 17, 18):
        hop(k)
    product_of(y, 0)
    product_of(ym, 1)
    n[14].wait_recv()
    n[15].wait_recv()
    values_of(b_o, 0, xl)
    product_of(yp, 2)
    for k in (10, 11, 16, 17):
        n[k].wait_recv()
    values_of(pi_of(yo, ol), 0, ol)
    product_of(yo, 0)

    for h in range(HEADS):
        tot[h] = 1.0 / tot[h]

    def out_rows(g, _):
        for a in range(4):
            s = g * 4 + a
            pieces = []
            for h in range(HEADS):
                rows = slice(h * SPAN, (h + 1) * SPAN)
                share = tot[h, 0:1, :]
                pieces.append((gate[s, rows, :] * (acc[s, rows, :] * share)).astype(BF16))
            mixed = jnp.concatenate(pieces, axis=0)
            out_ref[s] = jnp.dot(cw_ref[...], mixed, preferred_element_type=F32).astype(BF16)
        return 0

    lax.fori_loop(0, ROWS // 4, out_rows, 0)

    for c in n + e[0] + e[1]:
        c.wait_send()
    for r in range(2):
        for d in range(1, 16):
            m_copy(r, d).wait_send()


def body(duo, w, msa, gain, shift, pw, sw, cw):
    vm = pl.BlockSpec(memory_space=pltpu.VMEM)
    return pl.pallas_call(
        kernel,
        out_shape=jax.ShapeDtypeStruct((ROWS, CH, TOK), BF16),
        in_specs=[pl.BlockSpec(memory_space=pl.ANY)] + [vm] * 7,
        out_specs=vm,
        scratch_shapes=[
            pltpu.VMEM((8, ROWS, CH, TOK), BF16),
            pltpu.VMEM((4, HEADS, 2 * TOK, TOK), BF16),
            pltpu.VMEM((256 * HEADS, 128), F32),
            pltpu.VMEM((2, 16, HEADS, 128), F32),
            pltpu.VMEM((ROWS, 256, TOK), F32),
            pltpu.VMEM((ROWS, 256, TOK), F32),
            pltpu.VMEM((3 * 128, 256, 128), BF16),
            pltpu.VMEM((HEADS, 8, TOK), F32),
            pltpu.VMEM((256, CH), BF16),
            pltpu.VMEM((256, CH), BF16),
            pltpu.VMEM((2, CH, TOK), F32),
            pltpu.SemaphoreType.DMA((NPIECES,)),
            pltpu.SemaphoreType.DMA((18,)),
            pltpu.SemaphoreType.DMA((18,)),
            pltpu.SemaphoreType.DMA((2, 19)),
            pltpu.SemaphoreType.DMA((2, 19)),
            pltpu.SemaphoreType.DMA((2, 15)),
            pltpu.SemaphoreType.DMA((2, 15)),
        ],
        compiler_params=pltpu.CompilerParams(
            collective_id=0, has_side_effects=True, vmem_limit_bytes=66_800_000
        ),
        name="pair_average",
    )(duo.reshape(128, 256, 128), w.T, msa, gain.reshape(1, CH), shift.reshape(1, CH), pw, sw, cw.T)


def solution(mesh):
    placed = (P("pi", "pj", None), P(), P("pj", None, "pi"), P(), P(), P(), P(), P())
    return jax.shard_map(
        body, mesh=mesh, in_specs=placed, out_specs=P("pj", None, "pi"), check_vma=False
    )
```

time: 144 us -> 90.3 us (0.63)
  Pallas kernels: 140 us -> 87.8 us
  local copies, waits for them, and re-layouts: 3.79 us -> 2.3 us
    pallas_call x1, Pallas kernels: 140 us -> 87.8 us  [body(): pl.pallas_call(kernel, out_shape=jax.ShapeDtypeStruct((ROWS, CH, TOK), BF...]
    unnamed x2 -> x1, local copies, waits for them, and re-layouts: 3.79 us -> 2.3 us
where the time goes in v2:
time: 90.3 us; the launch traced here: 90.1 us
  Pallas kernels  87.8 us (97%)
  local copies, waits for them, and re-layouts  2.3 us (3%)
    pallas_call x1, Pallas kernels, body(): pl.pallas_call(kernel, out_shape=jax.ShapeDtypeStruct((ROWS, CH, TOK), BF...  87.8 us
    unnamed x1, local copies, waits for them, and re-layouts  2.3 us

profile of v2, /device:TPU:1, one launch (start us, length us, event | category | flops | bytes accessed | tf_op | source)
XLA Modules:
  0.0 90.1 jit_solution(18044266544291332403)
XLA Ops:
  0.0 87.8 %pair_average.1 = bf16[32,64,256]{2,1,0:T(8,128)(2,1)} custom-call(bf16[128,256,128]{2,1,0:T(8,128)(2,1)} %bitcast.5, f32[8,128]{1,0:T(8,128)} %bitcast.7, bf16[32,64,256]{2,1,0:T(8,128)(2,1)} %msa_ref.1, f32[1,64]{1,0:T(1,128)} %bitcast.8, f32[1,64]{1,0:T(1,128)} %bitcast.9, bf16[64,256]{1,0:T(8,128)(2,1)} %pw_ref.1, bf16[64,256]{1,0:T(8,128)(2,1)} %sw_ref.1, ...), custom_call_target="tpu_custom_call" | custom-call | tf_op jit(solution)/shard_map/pair_average/pallas_call | solution.py:377
  87.8 2.3 %copy.10 = bf16[32,64,256]{2,1,0:T(8,128)(2,1)} copy(bf16[32,64,256]{2,1,0:T(8,128)(2,1)} %pair_average.1) | data formatting | bytes 2097152

commit v3 on v2

--- a/solution.py
+++ b/solution.py
@@ -43,6 +43,8 @@
     yp, ym, yo = lax.rem(y + 1, 4), lax.rem(y + 3, 4), lax.rem(y + 2, 4)
     zp, zm, zo = lax.rem(z + 1, 4), lax.rem(z + 3, 4), lax.rem(z + 2, 4)
     ol, oh = 1 - xl, 1 - xh
+    y1, y3 = y + 1 - 2 * lax.rem(y, 2), 3 - y
+    swap = lax.rem(lax.div(y, 2) + xh, 2)
 
     step = 128 // NPIECES
 
@@ -102,7 +104,7 @@
     b_m, b_p, b_o = pi_of(ym, xl), pi_of(yp, xl), pi_of(yo, xl)
     q_m, q_p = pi_of(ym, ol), pi_of(yp, ol)
     n = [
-        n_copy(0, own, 0, xb, y, ol),
+        n_copy(0, own, 0, 6, y, ol),
         n_copy(1, own, xb, yb, y, ol),
         n_copy(2, own, xb, yb, yp, xl),
         n_copy(3, own, 0, xb, yp, xl),
@@ -110,8 +112,8 @@
         n_copy(5, own, 0, xb, ym, xl),
         n_copy(6, b_m, xb, ya, yp, xl),
         n_copy(7, b_p, ya, yb, ym, xl),
-        n_copy(8, b_m, xb, yb, y, ol),
-        n_copy(9, b_p, xb, yb, y, ol),
+        n_copy(8, pi_of(y3, xl), xb, yb, y, ol),
+        n_copy(9, pi_of(y1, xl), xb, yb, y, ol),
         n_copy(10, b_o, xb, ya, y, ol),
         n_copy(11, b_o, ya, yb, y, ol),
         n_copy(12, part, 0, xb, yp, xl),
@@ -120,6 +122,8 @@
         n_copy(15, b_p, xa, xb, ym, xl),
         n_copy(16, q_m, 0, xa, yp, xl),
         n_copy(17, q_p, xa, xb, ym, xl),
+        n_copy(18, own, 6, 14, y, ol),
+        n_copy(19, own, 14, xb, y, ol),
     ]
     for k in (2, 4, 0, 3, 5):
         n[k].start()
@@ -240,22 +244,6 @@
         for r in range(2)
     ]
 
-    scores_of(0)
-    scores_of(1)
-    n[2].wait_recv()
-    n[6].start()
-    n[4].wait_recv()
-    n[7].start()
-    for r in range(2):
-        exps_of(r)
-        for k in (2, 3, 1, 0):
-            e[r][k].start()
-    for k in (1, 8, 9):
-        n[k].start()
-
-    acc[...] = jnp.zeros_like(acc)
-    tot[...] = jnp.zeros_like(tot)
-
     def gate_rows(g, _):
         for a in range(4):
             s = g * 4 + a
@@ -266,8 +254,8 @@
     ones_t = jnp.ones((16, 2 * TOK), BF16)
 
     def value_rows(p, slot, c, g, _):
-        for a in range(8):
-            s = g * 8 + a
+        for a in range(16):
+            s = g * 16 + a
             v = jnp.dot(pwt[...], nbuf[p, s], preferred_element_type=F32).astype(BF16)
             vbuf[slot * 128 + s * 4 + c * 2] = v[:, 0:128]
             vbuf[slot * 128 + s * 4 + c * 2 + 1] = v[:, 128:256]
@@ -289,64 +277,93 @@
         return 0
 
     def values_of(p, slot, c):
-        lax.fori_loop(0, ROWS // 8, functools.partial(value_rows, p, slot, c), 0)
+        lax.fori_loop(0, ROWS // 16, functools.partial(value_rows, p, slot, c), 0)
 
     def product_of(yy, slot):
         lax.fori_loop(0, HEADS // 2, functools.partial(head_step, yy, slot), 0)
 
+    def hop(r, k, *then):
+        e[r][k].wait_recv()
+        for t in then:
+            e[r][t].start()
+
+    scores_of(0)
+    n[18].start()
+    scores_of(1)
+    exps_of(0)
+    for k in (2, 3, 1, 0):
+        e[0][k].start()
+    n[19].start()
+    n[2].wait_recv()
+    n[6].start()
+    n[4].wait_recv()
+    n[7].start()
     lax.fori_loop(0, ROWS // 4, gate_rows, 0)
+    exps_of(1)
+    for k in (2, 3, 1, 0):
+        e[1][k].start()
+    for k in (1, 8, 9):
+        n[k].start()
+    acc[...] = jnp.zeros_like(acc)
+    tot[...] = jnp.zeros_like(tot)
     values_of(own, 0, xl)
-
-    def hop(k, *then):
-        for r in range(2):
-            e[r][k].wait_recv()
-            for t in then:
-                e[r][t].start()
-
-    n[0].wait_recv()
+    hop(0, 2, 7, 8)
+    hop(0, 3, 9, 10)
+    for k in (0, 18, 19):
+        n[k].wait_recv()
     n[12].start()
     n[13].start()
-    hop(2, 7, 8)
-    hop(3, 9, 10)
+    hop(0, 1, 4, 5, 6)
+    hop(1, 2, 7, 8)
+    hop(1, 3, 9, 10)
     n[3].wait_recv()
     n[14].start()
     n[5].wait_recv()
     n[15].start()
+    values_of(pi_of(y3, xl), 2, xl)
+    hop(1, 1, 4, 5, 6)
     n[6].wait_recv()
     n[10].start()
     n[7].wait_recv()
     n[11].start()
-    hop(1, 4, 5, 6)
-    values_of(b_m, 1, xl)
-    hop(7, 11)
-    hop(9, 12)
-    values_of(b_p, 2, xl)
+    hop(0, 7, 11)
+    hop(0, 9, 12)
+    values_of(pi_of(y1, xl), 1, xl)
+    hop(1, 7, 11)
+    hop(1, 9, 12)
     n[1].wait_recv()
     values_of(part, 0, ol)
-    hop(4, 13, 14)
-    hop(5, 15, 16)
+    hop(0, 4, 13, 14)
+    hop(0, 5, 15, 16)
+    hop(1, 4, 13, 14)
+    hop(1, 5, 15, 16)
     n[12].wait_recv()
     n[16].start()
     n[13].wait_recv()
     n[17].start()
     n[8].wait_recv()
-    values_of(q_m, 1, ol)
+    values_of(pi_of(y3, ol), 2, ol)
+    for r in range(2):
+        for k in (0, 8, 10, 11, 12):
+            e[r][k].wait_recv()
+    product_of(y * (1 - swap) + y3 * swap, 2 * swap)
+    for r in range(2):
+        hop(r, 13, 17)
+        hop(r, 15, 18)
+    for r in range(2):
+        for k in (6, 14, 16, 17, 18):
+            e[r][k].wait_recv()
+    product_of(y3 * (1 - swap) + y * swap, 2 - 2 * swap)
     n[9].wait_recv()
-    values_of(q_p, 2, ol)
-    hop(13, 17)
-    hop(15, 18)
-    for k in (0, 8, 10, 11, 12, 6, 14, 16, 17, 18):
-        hop(k)
-    product_of(y, 0)
-    product_of(ym, 1)
+    values_of(pi_of(y1, ol), 1, ol)
+    product_of(y1, 1)
     n[14].wait_recv()
     n[15].wait_recv()
-    values_of(b_o, 0, xl)
-    product_of(yp, 2)
+    values_of(b_o, 2 * swap, xl)
     for k in (10, 11, 16, 17):
         n[k].wait_recv()
-    values_of(pi_of(yo, ol), 0, ol)
-    product_of(yo, 0)
+    values_of(pi_of(yo, ol), 2 * swap, ol)
+    product_of(yo, 2 * swap)
 
     for h in range(HEADS):
         tot[h] = 1.0 / tot[h]
@@ -392,8 +409,8 @@
             pltpu.VMEM((256, CH), BF16),
             pltpu.VMEM((2, CH, TOK), F32),
             pltpu.SemaphoreType.DMA((NPIECES,)),
-            pltpu.SemaphoreType.DMA((18,)),
-            pltpu.SemaphoreType.DMA((18,)),
+            pltpu.SemaphoreType.DMA((20,)),
+            pltpu.SemaphoreType.DMA((20,)),
             pltpu.SemaphoreType.DMA((2, 19)),
             pltpu.SemaphoreType.DMA((2, 19)),
             pltpu.SemaphoreType.DMA((2, 15)),

time: 90.3 us -> 82 us (0.908)
  Pallas kernels: 87.8 us -> 79.6 us
    pallas_call x1, Pallas kernels: 87.8 us -> 79.6 us  [body(): pl.pallas_call(kernel, out_shape=jax.ShapeDtypeStruct((ROWS, CH, TOK), BF...]
where the time goes in v3:
time: 82 us; the launch traced here: 81.9 us
  Pallas kernels  79.6 us (97%)
  local copies, waits for them, and re-layouts  2.3 us (3%)
    pallas_call x1, Pallas kernels, body(): pl.pallas_call(kernel, out_shape=jax.ShapeDtypeStruct((ROWS, CH, TOK), BF...  79.6 us
    unnamed x1, local copies, waits for them, and re-layouts  2.3 us

profile of v3, /device:TPU:1, one launch (start us, length us, event | category | flops | bytes accessed | tf_op | source)
XLA Modules:
  0.0 81.9 jit_solution(18256832038790408816)
XLA Ops:
  0.0 79.6 %pair_average.1 = bf16[32,64,256]{2,1,0:T(8,128)(2,1)} custom-call(bf16[128,256,128]{2,1,0:T(8,128)(2,1)} %bitcast.5, f32[8,128]{1,0:T(8,128)} %bitcast.7, bf16[32,64,256]{2,1,0:T(8,128)(2,1)} %msa_ref.1, f32[1,64]{1,0:T(1,128)} %bitcast.8, f32[1,64]{1,0:T(1,128)} %bitcast.9, bf16[64,256]{1,0:T(8,128)(2,1)} %pw_ref.1, bf16[64,256]{1,0:T(8,128)(2,1)} %sw_ref.1, ...), custom_call_target="tpu_custom_call" | custom-call | tf_op jit(solution)/shard_map/pair_average/pallas_call | solution.py:394
  79.6 2.3 %copy.10 = bf16[32,64,256]{2,1,0:T(8,128)(2,1)} copy(bf16[32,64,256]{2,1,0:T(8,128)(2,1)} %pair_average.1) | data formatting | bytes 2097152

commit v4 on v3

--- a/solution.py
+++ b/solution.py
@@ -18,8 +18,9 @@
 ROWS = 32
 CH = 64
 TOK = 256
-X_ROWS = 22
+X_ROWS = 21
 NPIECES = 8
+H_UNROLL = 8
 
 
 def kernel(
@@ -251,7 +252,7 @@
             gate[s] = jax.nn.sigmoid(t)
         return 0
 
-    ones_t = jnp.ones((16, 2 * TOK), BF16)
+    mine, other = pl.multiple_of(xl * TOK, TOK), pl.multiple_of(ol * TOK, TOK)
 
     def value_rows(p, slot, c, g, _):
         for a in range(16):
@@ -261,26 +262,31 @@
             vbuf[slot * 128 + s * 4 + c * 2 + 1] = v[:, 128:256]
         return 0
 
-    def head_step(yy, slot, g, _):
+    def head_step(yy, slot, classes, g, _):
         v4 = vbuf.at[pl.ds(slot * 128, 128)]
-        for a in range(2):
-            h = g * 2 + a
+        depth = len(classes) * TOK
+        for a in range(H_UNROLL):
+            h = g * H_UNROLL + a
             rows = pl.ds(pl.multiple_of(h * SPAN, SPAN), SPAN)
-            weights = ebuf[yy, h]
+            weights = [ebuf[yy, h, pl.ds((mine, other)[c], TOK), :] for c in classes]
+            weights = weights[0] if len(classes) == 1 else jnp.concatenate(weights, axis=0)
             v = v4[:, rows, :].reshape(ROWS, 4, SPAN, 128)
             v = jnp.concatenate(
-                [v[:, t].reshape(ROWS * SPAN, 128) for t in range(4)], axis=1
+                [v[:, 2 * c + t].reshape(ROWS * SPAN, 128) for c in classes for t in range(2)],
+                axis=1,
             )
+            v = jnp.concatenate([v, jnp.ones((16, depth), BF16)], axis=0)
             part_sum = jnp.dot(v, weights, preferred_element_type=F32)
-            acc[:, rows, :] += part_sum.reshape(ROWS, SPAN, TOK)
-            tot[h] += jnp.dot(ones_t, weights, preferred_element_type=F32)[0:8]
+            acc[:, rows, :] += part_sum[:ROWS * SPAN].reshape(ROWS, SPAN, TOK)
+            tot[h] += part_sum[ROWS * SPAN:ROWS * SPAN + 8]
         return 0
 
     def values_of(p, slot, c):
         lax.fori_loop(0, ROWS // 16, functools.partial(value_rows, p, slot, c), 0)
 
-    def product_of(yy, slot):
-        lax.fori_loop(0, HEADS // 2, functools.partial(head_step, yy, slot), 0)
+    def product_of(yy, slot, classes=(0, 1)):
+        step = functools.partial(head_step, yy, slot, classes)
+        lax.fori_loop(0, HEADS // H_UNROLL, step, 0)
 
     def hop(r, k, *then):
         e[r][k].wait_recv()
@@ -306,7 +312,7 @@
         n[k].start()
     acc[...] = jnp.zeros_like(acc)
     tot[...] = jnp.zeros_like(tot)
-    values_of(own, 0, xl)
+    values_of(own, 0, 0)
     hop(0, 2, 7, 8)
     hop(0, 3, 9, 10)
     for k in (0, 18, 19):
@@ -320,7 +326,7 @@
     n[14].start()
     n[5].wait_recv()
     n[15].start()
-    values_of(pi_of(y3, xl), 2, xl)
+    values_of(pi_of(y3, xl), 2, 0)
     hop(1, 1, 4, 5, 6)
     n[6].wait_recv()
     n[10].start()
@@ -328,13 +334,17 @@
     n[11].start()
     hop(0, 7, 11)
     hop(0, 9, 12)
-    values_of(pi_of(y1, xl), 1, xl)
+    values_of(pi_of(y1, xl), 1, 0)
     hop(1, 7, 11)
     hop(1, 9, 12)
     n[1].wait_recv()
-    values_of(part, 0, ol)
+    values_of(part, 0, 1)
     hop(0, 4, 13, 14)
     hop(0, 5, 15, 16)
+    for r in range(2):
+        for k in (0, 8, 10, 11, 12):
+            e[r][k].wait_recv()
+    product_of(y * (1 - swap) + y3 * swap, 2 * swap, (0,))
     hop(1, 4, 13, 14)
     hop(1, 5, 15, 16)
     n[12].wait_recv()
@@ -342,11 +352,8 @@
     n[13].wait_recv()
     n[17].start()
     n[8].wait_recv()
-    values_of(pi_of(y3, ol), 2, ol)
-    for r in range(2):
-        for k in (0, 8, 10, 11, 12):
-            e[r][k].wait_recv()
-    product_of(y * (1 - swap) + y3 * swap, 2 * swap)
+    values_of(pi_of(y3, ol), 2, 1)
+    product_of(y * (1 - swap) + y3 * swap, 2 * swap, (1,))
     for r in range(2):
         hop(r, 13, 17)
         hop(r, 15, 18)
@@ -355,22 +362,23 @@
             e[r][k].wait_recv()
     product_of(y3 * (1 - swap) + y * swap, 2 - 2 * swap)
     n[9].wait_recv()
-    values_of(pi_of(y1, ol), 1, ol)
+    values_of(pi_of(y1, ol), 1, 1)
     product_of(y1, 1)
     n[14].wait_recv()
     n[15].wait_recv()
-    values_of(b_o, 2 * swap, xl)
+    values_of(b_o, 2 * swap, 0)
+    product_of(yo, 2 * swap, (0,))
     for k in (10, 11, 16, 17):
         n[k].wait_recv()
-    values_of(pi_of(yo, ol), 2 * swap, ol)
-    product_of(yo, 2 * swap)
+    values_of(pi_of(yo, ol), 2 * swap, 1)
+    product_of(yo, 2 * swap, (1,))
 
     for h in range(HEADS):
         tot[h] = 1.0 / tot[h]
 
     def out_rows(g, _):
-        for a in range(4):
-            s = g * 4 + a
+        for a in range(8):
+            s = g * 8 + a
             pieces = []
             for h in range(HEADS):
                 rows = slice(h * SPAN, (h + 1) * SPAN)
@@ -380,7 +388,7 @@
             out_ref[s] = jnp.dot(cw_ref[...], mixed, preferred_element_type=F32).astype(BF16)
         return 0
 
-    lax.fori_loop(0, ROWS // 4, out_rows, 0)
+    lax.fori_loop(0, ROWS // 8, out_rows, 0)
 
     for c in n + e[0] + e[1]:
         c.wait_send()
@@ -393,7 +401,7 @@
     vm = pl.BlockSpec(memory_space=pltpu.VMEM)
     return pl.pallas_call(
         kernel,
-        out_shape=jax.ShapeDtypeStruct((ROWS, CH, TOK), BF16),
+        out_shape=pltpu.VMEM((ROWS, CH, TOK), BF16),
         in_specs=[pl.BlockSpec(memory_space=pl.ANY)] + [vm] * 7,
         out_specs=vm,
         scratch_shapes=[
@@ -417,7 +425,7 @@
             pltpu.SemaphoreType.DMA((2, 15)),
         ],
         compiler_params=pltpu.CompilerParams(
-            collective_id=0, has_side_effects=True, vmem_limit_bytes=66_800_000
+            collective_id=0, has_side_effects=True, vmem_limit_bytes=65_000_000
         ),
         name="pair_average",
     )(duo.reshape(128, 256, 128), w.T, msa, gain.reshape(1, CH), shift.reshape(1, CH), pw, sw, cw.T)

time: 82 us -> 75.9 us (0.926)
  Pallas kernels: 79.6 us -> 74.7 us
  local copies, waits for them, and re-layouts: 2.3 us -> 0.97 us
    pallas_call x1, Pallas kernels: 79.6 us -> 74.7 us  [body(): pl.pallas_call(kernel, out_shape=pltpu.VMEM((ROWS, CH, TOK), BF16), in_sp...]
    unnamed x1, local copies, waits for them, and re-layouts: 2.3 us -> 0.97 us
where the time goes in v4:
time: 75.9 us; the launch traced here: 75.7 us
  Pallas kernels  74.7 us (98%)
  local copies, waits for them, and re-layouts  0.97 us (1%)
    pallas_call x1, Pallas kernels, body(): pl.pallas_call(kernel, out_shape=pltpu.VMEM((ROWS, CH, TOK), BF16), in_sp...  74.7 us

profile of v4, /device:TPU:1, one launch (start us, length us, event | category | flops | bytes accessed | tf_op | source)
XLA Modules:
  0.0 75.7 jit_solution(5226632335666935922)
XLA Ops:
  0.0 74.7 %pair_average.1 = bf16[32,64,256]{2,1,0:T(8,128)(2,1)S(1)} custom-call(bf16[128,256,128]{2,1,0:T(8,128)(2,1)} %bitcast.5, f32[8,128]{1,0:T(8,128)} %bitcast.7, bf16[32,64,256]{2,1,0:T(8,128)(2,1)} %msa_ref.1, f32[1,64]{1,0:T(1,128)} %bitcast.8, f32[1,64]{1,0:T(1,128)} %bitcast.9, bf16[64,256]{1,0:T(8,128)(2,1)} %pw_ref.1, bf16[64,256]{1,0:T(8,128)(2,1)} %sw_ref.1, ...), custom_call_target="tpu_custom_call" | custom-call | tf_op jit(solution)/shard_map/pair_average/pallas_call | solution.py:402
  74.8 1.0 %copy.10 = bf16[32,64,256]{2,1,0:T(8,128)(2,1)} copy(bf16[32,64,256]{2,1,0:T(8,128)(2,1)S(1)} %pair_average.1) | data formatting | bytes 2097152

commit v5 on v4

--- a/solution.py
+++ b/solution.py
@@ -24,10 +24,10 @@
 
 
 def kernel(
-    duo_hbm, wt_ref, msa_ref, gain_ref, shift_ref, pw_ref, sw_ref, cw_ref,
+    duo_hbm, wt_ref, msa_hbm, gain_ref, shift_ref, pw_ref, sw_ref, cw_ref,
     out_ref,
-    nbuf, ebuf, sc, mx, acc, gate, vbuf, tot, pwt, swt, gcol,
-    duo_sem, n_send, n_recv, e_send, e_recv, m_send, m_recv,
+    msa, nbuf, ebuf, sc, mx, acc, gate, vbuf, tot, pwt, swt, gcol,
+    msa_sem, duo_sem, n_send, n_recv, e_send, e_recv, m_send, m_recv,
 ):
     pi = lax.axis_index("pi")
     pj = lax.axis_index("pj")
@@ -47,15 +47,20 @@
     y1, y3 = y + 1 - 2 * lax.rem(y, 2), 3 - y
     swap = lax.rem(lax.div(y, 2) + xh, 2)
 
+    def msa_copy(k, lo, hi):
+        rows = pl.ds(lo, hi - lo)
+        return pltpu.make_async_copy(msa_hbm.at[rows], msa.at[rows], msa_sem.at[k])
+
+    msa_in = [msa_copy(0, X_ROWS, ROWS), msa_copy(1, 0, X_ROWS)]
+    for c in msa_in:
+        c.start()
+
     step = 128 // NPIECES
 
     def duo_copy(k):
         rows = pl.ds(k * step, step)
         there = pl.ds(256 + k * step, step)
         return pltpu.make_async_copy(duo_hbm.at[rows], vbuf.at[there], duo_sem.at[k])
-
-    for k in range(NPIECES):
-        duo_copy(k).start()
 
     barrier = pltpu.get_barrier_semaphore()
     for d in range(1, 16):
@@ -67,6 +72,9 @@
             barrier, inc=1, device_id={"pi": other, "pj": pj}, device_id_type=MESH
         )
 
+    for k in range(NPIECES):
+        duo_copy(k).start()
+
     def column(ref):
         row = jnp.broadcast_to(ref[...], (CH, CH))
         r = lax.broadcasted_iota(jnp.int32, (CH, CH), 0)
@@ -77,19 +85,14 @@
     gcol[0] = column(gain_ref)
     gcol[1] = column(shift_ref)
 
-    def norm_rows(g, _):
-        for a in range(4):
-            s = g * 4 + a
-            v = msa_ref[s].astype(F32)
+    def norm_range(lo, hi):
+        for s in range(lo, hi):
+            v = msa[s].astype(F32)
             mean = jnp.mean(v, axis=0, keepdims=True)
             v = v - mean
             var = jnp.mean(v * v, axis=0, keepdims=True)
             v = v * lax.rsqrt(var + EPS)
             nbuf[pi, s] = (v * gcol[0] + gcol[1]).astype(BF16)
-        return 0
-
-    lax.fori_loop(0, ROWS // 4, norm_rows, 0)
-    pl.semaphore_wait(barrier, 18)
 
     xa, xb = X_ROWS // 2, X_ROWS
     ya, yb = X_ROWS + (ROWS - X_ROWS) // 2, ROWS
@@ -126,7 +129,16 @@
         n_copy(18, own, 6, 14, y, ol),
         n_copy(19, own, 14, xb, y, ol),
     ]
-    for k in (2, 4, 0, 3, 5):
+    msa_in[0].wait()
+    norm_range(X_ROWS, ROWS)
+    pl.semaphore_wait(barrier, 18)
+    for k in (2, 4):
+        n[k].start()
+    msa_in[1].wait()
+    norm_range(0, 6)
+    n[0].start()
+    norm_range(6, X_ROWS)
+    for k in (3, 5):
         n[k].start()
 
     pwt[...] = pw_ref[...].astype(F32).T.astype(BF16)
@@ -254,38 +266,44 @@
 
     mine, other = pl.multiple_of(xl * TOK, TOK), pl.multiple_of(ol * TOK, TOK)
 
-    def value_rows(p, slot, c, g, _):
-        for a in range(16):
-            s = g * 16 + a
+    def value_range(p, slot, c, lo, count):
+        for a in range(count):
+            s = lo + a
             v = jnp.dot(pwt[...], nbuf[p, s], preferred_element_type=F32).astype(BF16)
             vbuf[slot * 128 + s * 4 + c * 2] = v[:, 0:128]
             vbuf[slot * 128 + s * 4 + c * 2 + 1] = v[:, 128:256]
+
+    def value_half(p, slot, c, g, _):
+        value_range(p, slot, c, g * 16, 16)
         return 0
 
-    def head_step(yy, slot, classes, g, _):
-        v4 = vbuf.at[pl.ds(slot * 128, 128)]
+    def head_step(yy, slot, classes, lo, hi, with_total, g, _):
+        n_rows = hi - lo
+        v4 = vbuf.at[pl.ds(slot * 128 + lo * 4, n_rows * 4)]
         depth = len(classes) * TOK
         for a in range(H_UNROLL):
             h = g * H_UNROLL + a
             rows = pl.ds(pl.multiple_of(h * SPAN, SPAN), SPAN)
             weights = [ebuf[yy, h, pl.ds((mine, other)[c], TOK), :] for c in classes]
             weights = weights[0] if len(classes) == 1 else jnp.concatenate(weights, axis=0)
-            v = v4[:, rows, :].reshape(ROWS, 4, SPAN, 128)
+            v = v4[:, rows, :].reshape(n_rows, 4, SPAN, 128)
             v = jnp.concatenate(
-                [v[:, 2 * c + t].reshape(ROWS * SPAN, 128) for c in classes for t in range(2)],
+                [v[:, 2 * c + t].reshape(n_rows * SPAN, 128) for c in classes for t in range(2)],
                 axis=1,
             )
-            v = jnp.concatenate([v, jnp.ones((16, depth), BF16)], axis=0)
+            if with_total:
+                v = jnp.concatenate([v, jnp.ones((16, depth), BF16)], axis=0)
             part_sum = jnp.dot(v, weights, preferred_element_type=F32)
-            acc[:, rows, :] += part_sum[:ROWS * SPAN].reshape(ROWS, SPAN, TOK)
-            tot[h] += part_sum[ROWS * SPAN:ROWS * SPAN + 8]
+            acc[lo:hi, rows, :] += part_sum[:n_rows * SPAN].reshape(n_rows, SPAN, TOK)
+            if with_total:
+                tot[h] += part_sum[n_rows * SPAN:n_rows * SPAN + 8]
         return 0
 
     def values_of(p, slot, c):
-        lax.fori_loop(0, ROWS // 16, functools.partial(value_rows, p, slot, c), 0)
-
-    def product_of(yy, slot, classes=(0, 1)):
-        step = functools.partial(head_step, yy, slot, classes)
+        lax.fori_loop(0, ROWS // 16, functools.partial(value_half, p, slot, c), 0)
+
+    def product_of(yy, slot, classes=(0, 1), lo=0, hi=ROWS, with_total=True):
+        step = functools.partial(head_step, yy, slot, classes, lo, hi, with_total)
         lax.fori_loop(0, HEADS // H_UNROLL, step, 0)
 
     def hop(r, k, *then):
@@ -361,34 +379,39 @@
         for k in (6, 14, 16, 17, 18):
             e[r][k].wait_recv()
     product_of(y3 * (1 - swap) + y * swap, 2 - 2 * swap)
+    product_of(y1, 1, (0,))
     n[9].wait_recv()
     values_of(pi_of(y1, ol), 1, 1)
-    product_of(y1, 1)
+    product_of(y1, 1, (1,))
     n[14].wait_recv()
     n[15].wait_recv()
     values_of(b_o, 2 * swap, 0)
     product_of(yo, 2 * swap, (0,))
-    for k in (10, 11, 16, 17):
-        n[k].wait_recv()
-    values_of(pi_of(yo, ol), 2 * swap, 1)
-    product_of(yo, 2 * swap, (1,))
-
-    for h in range(HEADS):
-        tot[h] = 1.0 / tot[h]
-
-    def out_rows(g, _):
-        for a in range(8):
-            s = g * 8 + a
-            pieces = []
+
+    def out_row(s):
+        pieces = []
+        for h in range(HEADS):
+            rows = slice(h * SPAN, (h + 1) * SPAN)
+            share = tot[h, 0:1, :]
+            pieces.append((gate[s, rows, :] * (acc[s, rows, :] * share)).astype(BF16))
+        mixed = jnp.concatenate(pieces, axis=0)
+        out_ref[s] = jnp.dot(cw_ref[...], mixed, preferred_element_type=F32).astype(BF16)
+
+    def last_rows(lo, hi, first):
+        value_range(pi_of(yo, ol), 2 * swap, 1, lo, hi - lo)
+        product_of(yo, 2 * swap, (1,), lo, hi, first)
+        if first:
             for h in range(HEADS):
-                rows = slice(h * SPAN, (h + 1) * SPAN)
-                share = tot[h, 0:1, :]
-                pieces.append((gate[s, rows, :] * (acc[s, rows, :] * share)).astype(BF16))
-            mixed = jnp.concatenate(pieces, axis=0)
-            out_ref[s] = jnp.dot(cw_ref[...], mixed, preferred_element_type=F32).astype(BF16)
-        return 0
-
-    lax.fori_loop(0, ROWS // 8, out_rows, 0)
+                tot[h] = 1.0 / tot[h]
+        for s in range(lo, hi):
+            out_row(s)
+
+    n[16].wait_recv()
+    n[17].wait_recv()
+    last_rows(0, X_ROWS, True)
+    n[10].wait_recv()
+    n[11].wait_recv()
+    last_rows(X_ROWS, ROWS, False)
 
     for c in n + e[0] + e[1]:
         c.wait_send()
@@ -399,12 +422,14 @@
 
 def body(duo, w, msa, gain, shift, pw, sw, cw):
     vm = pl.BlockSpec(memory_space=pltpu.VMEM)
+    hbm = pl.BlockSpec(memory_space=pl.ANY)
     return pl.pallas_call(
         kernel,
         out_shape=pltpu.VMEM((ROWS, CH, TOK), BF16),
-        in_specs=[pl.BlockSpec(memory_space=pl.ANY)] + [vm] * 7,
+        in_specs=[hbm, vm, hbm] + [vm] * 5,
         out_specs=vm,
         scratch_shapes=[
+            pltpu.VMEM((ROWS, CH, TOK), BF16),
             pltpu.VMEM((8, ROWS, CH, TOK), BF16),
             pltpu.VMEM((4, HEADS, 2 * TOK, TOK), BF16),
             pltpu.VMEM((256 * HEADS, 128), F32),
@@ -416,6 +441,7 @@
             pltpu.VMEM((256, CH), BF16),
             pltpu.VMEM((256, CH), BF16),
             pltpu.VMEM((2, CH, TOK), F32),
+            pltpu.SemaphoreType.DMA((2,)),
             pltpu.SemaphoreType.DMA((NPIECES,)),
             pltpu.SemaphoreType.DMA((20,)),
             pltpu.SemaphoreType.DMA((20,)),

time: 75.9 us -> 74.7 us (0.984)
  Pallas kernels: 74.7 us -> 73.5 us
    pallas_call x1, Pallas kernels: 74.7 us -> 73.5 us  [body(): pl.pallas_call(kernel, out_shape=pltpu.VMEM((ROWS, CH, TOK), BF16), in_sp...]
where the time goes in v5:
time: 74.7 us; the launch traced here: 74.5 us
  Pallas kernels  73.5 us (98%)
  local copies, waits for them, and re-layouts  0.97 us (1%)
    pallas_call x1, Pallas kernels, body(): pl.pallas_call(kernel, out_shape=pltpu.VMEM((ROWS, CH, TOK), BF16), in_sp...  73.5 us

profile of v5, /device:TPU:1, one launch (start us, length us, event | category | flops | bytes accessed | tf_op | source)
XLA Modules:
  0.0 74.5 jit_solution(13774161898421840820)
XLA Ops:
  0.0 73.5 %pair_average.1 = bf16[32,64,256]{2,1,0:T(8,128)(2,1)S(1)} custom-call(bf16[128,256,128]{2,1,0:T(8,128)(2,1)} %bitcast.5, f32[8,128]{1,0:T(8,128)} %bitcast.7, bf16[32,64,256]{2,1,0:T(8,128)(2,1)} %msa_hbm.1, f32[1,64]{1,0:T(1,128)} %bitcast.8, f32[1,64]{1,0:T(1,128)} %bitcast.9, bf16[64,256]{1,0:T(8,128)(2,1)} %pw_ref.1, bf16[64,256]{1,0:T(8,128)(2,1)} %sw_ref.1, ...), custom_call_target="tpu_custom_call" | custom-call | tf_op jit(solution)/shard_map/pair_average/pallas_call | solution.py:426
  73.5 1.0 %copy.10 = bf16[32,64,256]{2,1,0:T(8,128)(2,1)} copy(bf16[32,64,256]{2,1,0:T(8,128)(2,1)S(1)} %pair_average.1) | data formatting | bytes 2097152

commit v6 on v5

--- a/solution.py
+++ b/solution.py
@@ -273,10 +273,6 @@
             vbuf[slot * 128 + s * 4 + c * 2] = v[:, 0:128]
             vbuf[slot * 128 + s * 4 + c * 2 + 1] = v[:, 128:256]
 
-    def value_half(p, slot, c, g, _):
-        value_range(p, slot, c, g * 16, 16)
-        return 0
-
     def head_step(yy, slot, classes, lo, hi, with_total, g, _):
         n_rows = hi - lo
         v4 = vbuf.at[pl.ds(slot * 128 + lo * 4, n_rows * 4)]
@@ -300,7 +296,7 @@
         return 0
 
     def values_of(p, slot, c):
-        lax.fori_loop(0, ROWS // 16, functools.partial(value_half, p, slot, c), 0)
+        value_range(p, slot, c, 0, ROWS)
 
     def product_of(yy, slot, classes=(0, 1), lo=0, hi=ROWS, with_total=True):
         step = functools.partial(head_step, yy, slot, classes, lo, hi, with_total)

time: 74.7 us -> 73.9 us (0.989)
    pallas_call x1, Pallas kernels: 73.5 us -> 72.8 us  [body(): pl.pallas_call(kernel, out_shape=pltpu.VMEM((ROWS, CH, TOK), BF16), in_sp...]
where the time goes in v6:
time: 73.9 us; the launch traced here: 73.8 us
  Pallas kernels  72.8 us (99%)
  local copies, waits for them, and re-layouts  0.97 us (1%)
    pallas_call x1, Pallas kernels, body(): pl.pallas_call(kernel, out_shape=pltpu.VMEM((ROWS, CH, TOK), BF16), in_sp...  72.8 us

profile of v6, /device:TPU:1, one launch (start us, length us, event | category | flops | bytes accessed | tf_op | source)
XLA Modules:
  0.0 73.8 jit_solution(9904419759409852590)
XLA Ops:
  0.0 72.8 %pair_average.1 = bf16[32,64,256]{2,1,0:T(8,128)(2,1)S(1)} custom-call(bf16[128,256,128]{2,1,0:T(8,128)(2,1)} %bitcast.5, f32[8,128]{1,0:T(8,128)} %bitcast.7, bf16[32,64,256]{2,1,0:T(8,128)(2,1)} %msa_hbm.1, f32[1,64]{1,0:T(1,128)} %bitcast.8, f32[1,64]{1,0:T(1,128)} %bitcast.9, bf16[64,256]{1,0:T(8,128)(2,1)} %pw_ref.1, bf16[64,256]{1,0:T(8,128)(2,1)} %sw_ref.1, ...), custom_call_target="tpu_custom_call" | custom-call | tf_op jit(solution)/shard_map/pair_average/pallas_call | solution.py:422
  72.8 1.0 %copy.10 = bf16[32,64,256]{2,1,0:T(8,128)(2,1)} copy(bf16[32,64,256]{2,1,0:T(8,128)(2,1)S(1)} %pair_average.1) | data formatting | bytes 2097152
